TPU v7x, 32 devices: a whole 2x2x4 slice. The times are simulated.
32 devices in a mesh: dom: 4 (over x, core), orb: 8 (over z, y).
Axes of the slice: x: 2, y: 2, z: 4, core: 2. Of those that a mesh axis runs over, the one named last changes fastest.
Arguments:
- orbitals: float32 [4, 16, 48, 2304], P('dom', 'orb'), may hold values from -6 to 6
- occupations: float32 [4, 16], P('dom', 'orb'), may hold values from 0.25 to 2
- occupied_count: int32 [4], P('dom'), may hold values from 4 to 16
- weights: float32 [4, 48], P('dom'), may hold values from 0 to 1, as said below
- external_potential: float32 [4, 48, 2304], P('dom'), may hold values from -2 to 0.5
- core_density: float32 [4, 48, 2304], P('dom'), may hold values from 0.08 to 2.88, as said below
- hartree_guess: float32 [128, 2304], P(('dom', 'orb')), may hold values from -6 to 6
Outputs:
- potential: float32 [128, 2304], P(('dom', 'orb'))
Inputs may be any that keep to these rules, and one draw needn't show every extreme that they name: orbitals 0 to occupied_count - 1 of a domain are occupied. `weights`: positive; on every global plane the weights of the boxes that cover it sum to one. `core_density`: positive.
All inputs are finite; a program needn't handle non-finite values.
Results may differ from a plain program's by a relative error of at most 0.00017.
Values sent between devices are 32-bit elements; how exact they have to be, the bound alone decides.
A program may use at most 64 MiB of HBM per device.

v0:
```python
import functools

import jax
import jax.numpy as jnp
from jax import lax
from jax.experimental import pallas as pl
from jax.experimental.pallas import tpu as pltpu
from jax.sharding import PartitionSpec as P

SIDE = 48
CORE = 32
BUF = 8
DEGREE = 8
SWEEPS = 4
CYCLES = 2


EXCHANGE_FACTOR = (3.0 / 3.141592653589793) ** (1.0 / 3.0)
FOUR_PI = 4.0 * 3.141592653589793
RELAXATION = 0.8
CUTOFF = 1.5


MESH = pl.DeviceIdType.MESH


def lane_neighbours(field, column):
    cells = field.shape[-1]
    left = jnp.where(
        column == 0, pltpu.roll(field, cells - (SIDE - 1), 1), pltpu.roll(field, 1, 1)
    )
    right = jnp.where(
        column == SIDE - 1, pltpu.roll(field, SIDE - 1, 1), pltpu.roll(field, cells - 1, 1)
    )
    return left + right + pltpu.roll(field, SIDE, 1) + pltpu.roll(field, cells - SIDE, 1)


def filtered_density(
    last, ranks, orbitals, factors, weight, core, ionic, scf, result, weighted,
    even, odd, diagonal, columns,
):
    count, box, cells = orbitals.shape
    planes = weighted.shape[1]
    blocks = box // 8
    if scf is None:
        diagonal[...] = ionic[...]
    else:
        for chunk in range(box // planes):
            rows = slice(chunk * planes, (chunk + 1) * planes)
            diagonal[rows, :] = ionic[rows, :] + scf[chunk]
    potential = diagonal[...]
    lowest = jnp.min(jnp.min(potential, axis=0, keepdims=True), axis=1, keepdims=True)
    highest = jnp.max(jnp.max(potential, axis=0, keepdims=True), axis=1, keepdims=True)
    low_bound = lowest + CUTOFF
    high_bound = highest + 6.0
    center = 0.5 * (high_bound + low_bound)
    inverse = 1.0 / (0.5 * (high_bound - low_bound))
    diagonal[...] = (2.0 * inverse) * ((3.0 - center) + potential)
    columns[...] = lax.broadcasted_iota(jnp.int32, columns.shape, 1) % SIDE
    edge = jnp.zeros((8, cells), jnp.float32)
    for orbital in range(count):
        for buffer in (even, odd):
            buffer[orbital, 0:8, :] = edge
            buffer[orbital, 8 + box : 16 + box, :] = edge
        even[orbital, 8 : 8 + box, :] = orbitals[orbital]
    sublane = lax.broadcasted_iota(jnp.int32, (8, cells), 0)

    def sweep(source, target, first):
        def at(block, carry):
            base = pl.multiple_of(8 * block, 8)
            middle_rows = pl.ds(base + 8, 8)
            scale = diagonal[pl.ds(base, 8), :]
            column = columns[...]
            values = []
            for orbital in range(count):
                middle = source[orbital, middle_rows, :]
                below = source[orbital, pl.ds(base, 8), :]
                above = source[orbital, pl.ds(base + 16, 8), :]
                near = pltpu.roll(jnp.where(sublane == 7, below, middle), 1, 0)
                near = near + pltpu.roll(jnp.where(sublane == 0, above, middle), 7, 0)
                near = near + lane_neighbours(middle, column)
                value = scale * middle - inverse * near
                if first:
                    value = 0.5 * value
                else:
                    value = value - target[orbital, middle_rows, :]
                values.append(value)
            for orbital in range(count):
                target[orbital, middle_rows, :] = values[orbital]
            return carry

        lax.fori_loop(0, blocks, at, 0, unroll=True)

    sweep(even, odd, True)

    def two_sweeps(step, carry):
        sweep(odd, even, False)
        sweep(even, odd, False)
        return carry

    lax.fori_loop(0, (DEGREE - 1) // 2, two_sweeps, 0)
    if DEGREE % 2 == 0:
        sweep(odd, even, False)
    final = even if DEGREE % 2 == 0 else odd
    shares = []
    for orbital in range(count):
        def squares_of(block, total):
            base = pl.multiple_of(8 * block, 8)
            value = final[orbital, pl.ds(base + 8, 8), :]
            value = value * value
            for lane in range(0, cells, 128):
                total = total + value[:, lane : lane + 128]
            return total

        total = lax.fori_loop(0, blocks, squares_of, jnp.zeros((8, 128), jnp.float32))
        total = jnp.sum(jnp.sum(total, axis=0, keepdims=True), axis=1, keepdims=True)
        squares = total * (1.0 / (box * cells)) + 1e-06
        shares.append(factors[0, orbital] / squares)
        if not last:
            result[orbital] = final[orbital, 8 : 8 + box, :] * (
                1.0 / jnp.sqrt(squares)
            )
    for block in range(blocks):
        rows = slice(8 * block, 8 * block + 8)
        density = core[rows, :] * (1.0 / ranks)
        for orbital in range(count):
            value = final[orbital, 8 + 8 * block : 16 + 8 * block, :]
            density = density + shares[orbital] * (value * value)
        density = density * weight[rows, :]
        for piece in range(8 // planes):
            weighted[block * (8 // planes) + piece] = density[
                piece * planes : (piece + 1) * planes, :
            ]


def cycle_kernel(last, has_scf, doms, ranks, *refs):
    orbitals, factors, weight, core, ionic, start = refs[:6]
    scf = refs[6] if has_scf else None
    refs = refs[7:] if has_scf else refs[6:]
    outs = 1 if last else 3
    outputs = refs[:outs]
    (
        weighted, even, odd, diagonal, columns,
        parts, near_h, near_d, work, work_d, own_pot, box_pot, sums, dom_sums,
        part_send, part_recv, h_send, h_recv, d_send, d_recv,
        sum_send, sum_recv, dom_send, dom_recv, box_send, box_recv,
    ) = refs[outs:]
    chunks, planes, cells = weighted.shape
    rim = BUF // planes
    reach = near_h.shape[0] // 2
    everyone = doms * ranks
    dom = lax.axis_index("dom")
    rank = lax.axis_index("orb")
    me = dom * ranks + rank
    in_low = rank < rim
    in_high = rank >= ranks - rim
    in_rim = jnp.logical_or(in_low, in_high)

    def place(index):
        return (lax.div(index, ranks), lax.rem(index, ranks))

    def send(source, target, send_sem, recv_sem, index):
        return pltpu.make_async_remote_copy(
            src_ref=source, dst_ref=target, send_sem=send_sem, recv_sem=recv_sem,
            device_id=index, device_id_type=MESH,
        )

    def repeat(low, high, step):
        lax.fori_loop(low, high, lambda i, carry: (step(i), carry)[1], 0)

    barrier = pltpu.get_barrier_semaphore()

    def greet(k):
        pl.semaphore_signal(
            barrier, inc=1, device_id=place(lax.rem(me + k, everyone)), device_id_type=MESH
        )

    repeat(1, everyone, greet)
    filtered_density(
        last, ranks, orbitals, factors, weight, core, ionic, scf,
        None if last else outputs[2], weighted, even, odd, diagonal, columns,
    )
    pl.semaphore_wait(barrier, everyone - 1)

    def part_copy(k):
        chunk = lax.rem(rank + rim + k, chunks)
        owner = lax.rem(dom * ranks + chunk - rim + everyone, everyone)
        to = place(owner)
        slot = jnp.where(to[0] == dom, rank, ranks + rank)
        return send(
            weighted.at[chunk], parts.at[slot], part_send.at[chunk], part_recv.at[slot], to
        )

    repeat(1, chunks, lambda k: part_copy(k).start())

    def near_copies(source, buffer, send_sems, recv_sems):
        copies = []
        for k in range(1, reach + 1):
            for sign in (1, -1):
                to = place(lax.rem(me + sign * k + everyone, everyone))
                slot = reach - sign * k
                copies.append(
                    send(source, buffer.at[slot], send_sems.at[slot], recv_sems.at[slot], to)
                )
        return copies

    h_copies = near_copies(start, near_h, h_send, h_recv)
    for copy in h_copies:
        copy.start()

    charge = weighted[0]
    for chunk in range(1, chunks):
        charge = charge + weighted[chunk]
    charge = jnp.sum(charge, axis=0, keepdims=True)
    row = charge[:, :128]
    for lane in range(128, cells, 128):
        row = row + charge[:, lane : lane + 128]
    sums[rank] = jnp.broadcast_to(row, (8, 128))

    def sum_copy(k):
        to = (dom, lax.rem(rank + k, ranks))
        return send(sums.at[rank], sums.at[rank], sum_send.at[k], sum_recv.at[rank], to)

    repeat(1, ranks, lambda k: sum_copy(k).start())

    def arrived(buffer, slot, sems):
        send(buffer.at[slot], buffer.at[slot], sems.at[slot], sems.at[slot], (dom, rank)).wait_recv()

    near_d[reach] = weighted[rank + rim]

    def take(slot):
        arrived(parts, slot, part_recv)
        near_d[reach] += parts[slot]

    repeat(1, ranks, lambda k: take(lax.rem(rank + k, ranks)))

    @pl.when(in_rim)
    def _():
        repeat(0, ranks, lambda k: take(ranks + lax.rem(rank + k, ranks)))

    d_copies = near_copies(near_d.at[reach], near_d, d_send, d_recv)
    for copy in d_copies:
        copy.start()

    repeat(1, ranks, lambda k: arrived(sums, lax.rem(rank + k, ranks), sum_recv))
    dom_sums[dom] = jnp.sum(sums[...], axis=0)

    def dom_copy(k):
        to = (lax.rem(dom + k, doms), rank)
        return send(dom_sums.at[dom], dom_sums.at[dom], dom_send.at[k], dom_recv.at[dom], to)

    repeat(1, doms, lambda k: dom_copy(k).start())

    work[...] = jnp.zeros_like(work)
    work_d[...] = jnp.zeros_like(work_d)
    near_h[reach] = start[...]
    for slot in range(2 * reach + 1):
        if slot != reach:
            arrived(near_h, slot, h_recv)
        work[slot * planes : (slot + 1) * planes, :] = near_h[slot]
    for slot in range(2 * reach + 1):
        if slot != reach:
            arrived(near_d, slot, d_recv)
        work_d[slot * planes : (slot + 1) * planes, :] = near_d[slot]

    field = work[...]
    source = FOUR_PI * work_d[...]
    rows = field.shape[0]
    column = lax.broadcasted_iota(jnp.int32, field.shape, 1) % SIDE
    for _ in range(SWEEPS):
        near = pltpu.roll(field, 1, 0) + pltpu.roll(field, rows - 1, 0)
        near = near + lane_neighbours(field, column)
        field = field + RELAXATION * ((near + source) * (1.0 / 6.0) - field)
    work[...] = field
    mine = work[reach * planes : (reach + 1) * planes, :]
    density = near_d[reach]
    root = jnp.exp(jnp.log(density) * (1.0 / 3.0))
    root = root - (root - density / (root * root)) * (1.0 / 3.0)
    own_pot[...] = mine - EXCHANGE_FACTOR * root

    def box_copy(k):
        to = (dom, lax.rem(rank + k, ranks))
        slot = rank + rim
        return send(own_pot, box_pot.at[slot], box_send.at[k], box_recv.at[slot], to)

    def rim_copy(k):
        to_dom = jnp.where(in_low, lax.rem(dom + doms - 1, doms), lax.rem(dom + 1, doms))
        slot = jnp.where(in_low, rank + ranks + rim, rank - ranks + rim)
        to = (to_dom, lax.rem(rank + k, ranks))
        return send(own_pot, box_pot.at[slot], box_send.at[ranks + k], box_recv.at[slot], to)

    if not last:
        repeat(1, ranks, lambda k: box_copy(k).start())

        @pl.when(in_rim)
        def _():
            repeat(0, ranks, lambda k: rim_copy(k).start())

    repeat(1, doms, lambda k: arrived(dom_sums, lax.rem(dom + k, doms), dom_recv))
    total = jnp.sum(jnp.sum(dom_sums[...], axis=0)[:1, :])
    average = total / (everyone * planes * cells)
    shift = (-SWEEPS * RELAXATION * FOUR_PI / 6.0) * average
    if last:
        outputs[0][...] = own_pot[...] + shift
    else:
        outputs[1][...] = mine + shift
        box_pot[rank + rim] = own_pot[...]
        repeat(
            1, chunks, lambda k: arrived(box_pot, lax.rem(rank + rim + k, chunks), box_recv)
        )
        outputs[0][...] = box_pot[...] + shift
        repeat(1, ranks, lambda k: box_copy(k).wait_send())

        @pl.when(in_rim)
        def _():
            repeat(0, ranks, lambda k: rim_copy(k).wait_send())

    repeat(1, chunks, lambda k: part_copy(k).wait_send())
    for copy in h_copies + d_copies:
        copy.wait_send()
    repeat(1, ranks, lambda k: sum_copy(k).wait_send())
    repeat(1, doms, lambda k: dom_copy(k).wait_send())


def run_cycle(orbitals, factors, weight, core, ionic, hartree, scf, last):
    doms, ranks = lax.axis_size("dom"), lax.axis_size("orb")
    count, box_planes, cells = orbitals.shape
    planes = hartree.shape[0]
    chunks = box_planes // planes
    reach = -(-SWEEPS // planes)
    span = 2 * reach + 1
    rows = -(-span * planes // 8) * 8
    f32 = jnp.float32
    box = jax.ShapeDtypeStruct((chunks, planes, cells), f32)
    own = jax.ShapeDtypeStruct((planes, cells), f32)
    vmem = pl.BlockSpec(memory_space=pltpu.VMEM)
    dma = pltpu.SemaphoreType.DMA
    operands = [orbitals, factors, weight, core, ionic, hartree]
    if scf is not None:
        operands.append(scf)
    specs = [vmem] * len(operands)
    specs[1] = pl.BlockSpec(memory_space=pltpu.SMEM)
    shapes = (own,) if last else (box, own, jax.ShapeDtypeStruct(orbitals.shape, f32))
    return pl.pallas_call(
        functools.partial(cycle_kernel, last, scf is not None, doms, ranks),
        out_shape=shapes,
        in_specs=specs,
        out_specs=(vmem,) * len(shapes),
        scratch_shapes=[
            pltpu.VMEM((chunks, planes, cells), f32),
            pltpu.VMEM((count, box_planes + 16, cells), f32),
            pltpu.VMEM((count, box_planes + 16, cells), f32),
            pltpu.VMEM((box_planes, cells), f32),
            pltpu.VMEM((8, cells), jnp.int32),
            pltpu.VMEM((2 * ranks, planes, cells), f32),
            pltpu.VMEM((span, planes, cells), f32),
            pltpu.VMEM((span, planes, cells), f32),
            pltpu.VMEM((rows, cells), f32),
            pltpu.VMEM((rows, cells), f32),
            pltpu.VMEM((planes, cells), f32),
            pltpu.VMEM((chunks, planes, cells), f32),
            pltpu.VMEM((ranks, 8, 128), f32),
            pltpu.VMEM((doms, 8, 128), f32),
            dma((chunks,)), dma((2 * ranks,)),
            dma((span,)), dma((span,)),
            dma((span,)), dma((span,)),
            dma((ranks,)), dma((ranks,)),
            dma((doms,)), dma((doms,)),
            dma((2 * ranks,)), dma((chunks,)),
        ],
        compiler_params=pltpu.CompilerParams(
            collective_id=1 if last else 0, has_side_effects=True
        ),
        name="cycle_last" if last else "cycle_first",
    )(*operands)


def body(
    orbitals, occupations, occupied_count, weights, external_potential, core_density, hartree_guess
):
    orb_count = lax.axis_size("orb")
    orb_rank = lax.axis_index("orb")
    per_device = orbitals.shape[1]
    orbital_rank = orb_rank * per_device + jnp.arange(per_device, dtype=jnp.int32)
    factors = jnp.where(orbital_rank < occupied_count[0], occupations[0], jnp.float32(0.0)) / (
        per_device * orb_count
    )
    factors = factors.reshape(1, per_device)
    box_weight = weights[0][:, None]
    orbital_set = orbitals[0]
    hartree = hartree_guess
    scf = None
    for cycle_index in range(CYCLES):
        last = cycle_index + 1 == CYCLES
        results = run_cycle(
            orbital_set, factors, box_weight, core_density[0], external_potential[0],
            hartree, scf, last,
        )
        if last:
            return results[0]
        scf, hartree, orbital_set = results


def solution(mesh):
    placed = (
        P("dom", "orb", None, None),
        P("dom", "orb"),
        P("dom"),
        P("dom", None),
        P("dom", None, None),
        P("dom", None, None),
        P(("dom", "orb"), None),
    )
    return jax.shard_map(
        body, mesh=mesh, in_specs=placed, out_specs=P(("dom", "orb"), None), check_vma=False
    )
```

profile of v0, /device:TPU:0, one launch (start us, length us, event | category | flops | bytes accessed | tf_op | source)
XLA Modules:
  0.0 91.6 jit_solution(14265688380679447434)
XLA Ops:
  0.7 0.0 copy-start.1
  0.7 0.6 copy-done.1
  1.3 0.5 fusion.refs_1_
  1.8 0.0 copy-start
  1.8 0.7 copy-done
  2.5 0.7 copy.8.refs_2_
  3.2 49.3 %cycle_first.1 = (f32[12,4,2304]{2,1,0:T(4,128)}, f32[4,2304]{1,0:T(4,128)}, f32[2,48,2304]{2,1,0:T(8,128)}) custom-call(f32[2,48,2304]{2,1,0:T(8,128)} %bitcast.10, f32[1,2]{1,0:T(1,128)} %fusion.refs_1_, f32[48,1]{1,0:T(8,128)} %copy.8.refs_2_, f32[48,2304]{1,0:T(8,128)} %bitcast.6, f32[48,2304]{1,0:T(8,128)} %bitcast.8, f32[4,2304]{1,0:T(4,128)} %refs_5_.1), custom_call_target="tpu_custom_call" | custom-call | tf_op jit(solution)/shard_map/cycle_first/pallas_call | solution.py:344
  52.5 37.7 %cycle_last.1 = f32[4,2304]{1,0:T(4,128)} custom-call(f32[2,48,2304]{2,1,0:T(8,128)} %get-tuple-element.8.refs_0_, f32[1,2]{1,0:T(1,128)} %fusion.refs_1_, f32[48,1]{1,0:T(8,128)} %copy.8.refs_2_, f32[48,2304]{1,0:T(8,128)} %bitcast.7, f32[48,2304]{1,0:T(8,128)} %bitcast.9, f32[4,2304]{1,0:T(4,128)} %get-tuple-element.9.refs_5_, ...), custom_call_target="tpu_custom_call" | custom-call | tf_op jit(solution)/shard_map/cycle_last/pallas_call | solution.py:344
  90.2 1.4 %copy.12 = f32[4,2304]{1,0:T(4,128)} copy(f32[4,2304]{1,0:T(4,128)} %cycle_last.1) | data formatting | bytes 73728
Async XLA Ops:
  0.7 0.7 copy-start.1
  1.8 0.7 copy-start
where the time goes:
time: 91.9 us; the launch traced here: 91.6 us
  Pallas kernels  87 us (95%)
  local copies, waits for them, and re-layouts  3.39 us (4%)
    pallas_call x2, Pallas kernels, run_cycle(): pl.pallas_call(functools.partial(cycle_kernel, last, scf is not None, dom...  87 us
    unnamed x5, local copies, waits for them, and re-layouts  2.69 us

commit v1 on v0

v1 whole, which is shorter than its diff:
```python
import functools

import jax
import jax.numpy as jnp
from jax import lax
from jax.experimental import pallas as pl
from jax.experimental.pallas import tpu as pltpu
from jax.sharding import PartitionSpec as P

SIDE = 48
BUF = 8
DEGREE = 8
SWEEPS = 4
CYCLES = 2
LANES = 128
HALF = 64
SEGMENTS = 4
GROUP = 4


EXCHANGE_FACTOR = (3.0 / 3.141592653589793) ** (1.0 / 3.0)
FOUR_PI = 4.0 * 3.141592653589793
RELAXATION = 0.8
CUTOFF = 1.5


MESH = pl.DeviceIdType.MESH


class Segments:
    def __init__(self, count, box, cells):
        self.count, self.box, self.cells = count, box, cells
        self.lines = cells // SIDE // SEGMENTS
        self.across = LANES // (SEGMENTS * count)
        self.deep = box // self.across
        self.length = self.lines * SIDE
        self.tiles = cells // LANES
        self.blocks = -(-self.length // LANES)
        self.shift = count * self.across
        assert self.deep * self.across == box and self.length % HALF == 0
        assert self.tiles * LANES == cells and SIDE % 8 == 0 and box % 8 == 0

    def spread(self, load, store):
        lane = lax.broadcasted_iota(jnp.int32, (self.across, LANES), 1)
        for plane in range(self.deep):
            kept = {}

            def tile_of(orbital, tile, turned):
                if (orbital, tile, turned) not in kept:
                    value = load(orbital, tile, plane)
                    kept[orbital, tile, turned] = pltpu.roll(value, HALF, 1) if turned else value
                return kept[orbital, tile, turned]

            for block in range(self.blocks):
                rows = min(LANES, self.length - block * LANES)
                pieces = []
                for segment in range(SEGMENTS):
                    first = segment * self.length + block * LANES
                    for orbital in range(self.count):
                        parts = []
                        for half in range(2):
                            cell = min(first + half * HALF, self.cells - HALF)
                            turned = cell % LANES != half * HALF
                            parts.append(tile_of(orbital, cell // LANES, turned))
                        if rows <= HALF or parts[0] is parts[1]:
                            pieces.append(parts[0])
                        else:
                            pieces.append(jnp.where(lane < HALF, parts[0], parts[1]))
                turned = jnp.concatenate(pieces, axis=0).T
                for row in range(0, rows, 8):
                    store(plane, block * LANES + row, turned[row : row + 8])

    def gather(self, load, store):
        lane = lax.broadcasted_iota(jnp.int32, (self.across, LANES), 1)
        for plane in range(self.deep):
            sums = {}
            for block in range(self.blocks):
                rows = min(LANES, self.length - block * LANES)
                pieces = [load(plane, block * LANES + row) for row in range(0, rows, 8)]
                if rows < LANES:
                    pieces.append(jnp.zeros((LANES - rows, LANES), jnp.float32))
                turned = jnp.concatenate(pieces, axis=0).T
                for segment in range(SEGMENTS):
                    base = segment * self.shift
                    value = turned[base : base + self.across]
                    for orbital in range(1, self.count):
                        at = base + orbital * self.across
                        value = value + turned[at : at + self.across]
                    sums[segment, block, False] = value

            def half_of(cell, half):
                segment, place = cell // self.length, cell % self.length
                turned = place % LANES != half * HALF
                key = (segment, place // LANES, turned)
                if key not in sums:
                    sums[key] = pltpu.roll(sums[key[0], key[1], False], HALF, 1)
                return sums[key]

            for tile in range(self.tiles):
                low = half_of(tile * LANES, 0)
                high = half_of(tile * LANES + HALF, 1)
                store(plane, tile, low if low is high else jnp.where(lane < HALF, low, high))


def filter_step(shape, source, target, scale, inverse, first):
    lines, deep, across = shape.lines, shape.deep, shape.across
    lane = lax.broadcasted_iota(jnp.int32, (1, 8, LANES), 2) % across
    has_left = jnp.broadcast_to(lane != 0, (GROUP, 8, LANES))
    has_right = jnp.broadcast_to(lane != across - 1, (GROUP, 8, LANES))

    def turn(value, amount):
        return pltpu.roll(value.reshape(-1, LANES), amount, 1).reshape(value.shape)

    for base in range(0, SIDE, 8):
        cells = slice(8 + base, 16 + base)

        def line(plane, at):
            return source[plane * lines + at : plane * lines + at + 1, cells, :]

        for start in range(0, lines, GROUP):
            middles = [
                source[plane * lines + start : plane * lines + start + GROUP, cells, :]
                for plane in range(deep)
            ]
            for plane in range(deep):
                block = slice(plane * lines + start, plane * lines + start + GROUP)
                middle = middles[plane]
                if plane > 0:
                    left = middles[plane - 1]
                else:
                    left = jnp.where(has_left, turn(middles[deep - 1], 1), 0.0)
                if plane < deep - 1:
                    right = middles[plane + 1]
                else:
                    right = jnp.where(has_right, turn(middles[0], LANES - 1), 0.0)
                if start > 0:
                    below = line(plane, start - 1)
                else:
                    below = turn(line(plane, lines - 1), shape.shift)
                if start + GROUP < lines:
                    above = line(plane, start + GROUP)
                else:
                    above = turn(line(plane, 0), LANES - shape.shift)
                below = jnp.concatenate([below, middle[:-1]], axis=0)
                above = jnp.concatenate([middle[1:], above], axis=0)
                near = source[block, 7 + base : 15 + base, :] + source[block, 9 + base : 17 + base, :]
                near = near + (below + above)
                near = near + (left + right)
                value = scale[block, base : base + 8, :] * middle - inverse * near
                if first:
                    value = 0.5 * value
                else:
                    value = value - target[block, cells, :]
                target[block, cells, :] = value
                if base == 0:
                    target[block, 8 + SIDE : 9 + SIDE, :] = value[:, :1, :]
                if base == SIDE - 8:
                    target[block, 7:8, :] = value[:, 7:, :]


def cycles_kernel(doms, ranks, *refs):
    (
        orbitals_hbm, occupations, counts, weights, ionic_hbm, core_hbm, hartree_hbm,
        output,
        planes_of, ionic, core, flat, weight_rows, even, odd, scale, charge,
        weighted, rim_in, parts, near_h, near_d, work, work_d, box_pot, sums, dom_sums,
        load_sem, rim_send, rim_recv, part_send, part_recv, h_send, h_recv, d_send, d_recv,
        sum_send, sum_recv, dom_send, dom_recv, box_send, box_recv, relay_send,
    ) = refs
    count, box, cells = orbitals_hbm.shape
    chunks, planes, _ = weighted.shape
    shape = Segments(count, box, cells)
    tiles = shape.tiles
    rim = BUF // planes
    reach = near_h.shape[1] // 2
    everyone = doms * ranks
    dom = lax.axis_index("dom")
    rank = lax.axis_index("orb")
    me = dom * ranks + rank

    def place(index):
        return (lax.div(index, ranks), lax.rem(index, ranks))

    def send(source, target, send_sem, recv_sem, to):
        return pltpu.make_async_remote_copy(
            src_ref=source, dst_ref=target, send_sem=send_sem, recv_sem=recv_sem,
            device_id=to, device_id_type=MESH,
        )

    def repeat(low, high, step):
        lax.fori_loop(low, high, lambda i, carry: (step(i), carry)[1], 0)

    def arrived(target, sem):
        send(target, target, sem, sem, (dom, rank)).wait_recv()

    def loads(source, target, sem):
        for tile in range(tiles):
            pltpu.make_async_copy(
                source.at[:, tile * LANES : (tile + 1) * LANES],
                target.at[tile],
                sem,
            ).start()

    def loaded(target, sem):
        pltpu.make_async_copy(target, target, sem).wait()

    loads(ionic_hbm, ionic, load_sem.at[0])
    for orbital in range(count):
        loads(orbitals_hbm.at[orbital], planes_of.at[orbital], load_sem.at[1 + orbital])
    guess = pltpu.make_async_copy(hartree_hbm, near_h.at[0, reach], load_sem.at[1 + count])
    guess.start()
    loads(core_hbm, core, load_sem.at[2 + count])

    barrier = pltpu.get_barrier_semaphore()

    def greet(k):
        pl.semaphore_signal(
            barrier, inc=1, device_id=place(lax.rem(me + k, everyone)), device_id_type=MESH
        )

    repeat(1, everyone, greet)

    sublane = lax.broadcasted_iota(jnp.int32, (8, LANES), 0)
    for group in range(0, box, 8):
        rows = jnp.full((8, LANES), weights[0, group], jnp.float32)
        for row in range(1, 8):
            rows = jnp.where(sublane == row, weights[0, group + row], rows)
        weight_rows[group : group + 8, :] = rows

    lane = lax.broadcasted_iota(jnp.int32, (8, LANES), 1)
    orbital_of = lax.rem(lax.div(lane, shape.across), count)

    def strided(ref, tile, plane):
        return ref[tile, pl.ds(plane, shape.across, stride=shape.deep), :]

    def place_of(plane, cell):
        return plane * shape.lines + cell // SIDE, cell % SIDE

    def store_orbitals(plane, cell, value):
        line, at = place_of(plane, cell)
        even[line, 8 + at : 16 + at, :] = value
        if at == 0:
            even[line, 8 + SIDE : 9 + SIDE, :] = value[:1]
        if at == SIDE - 8:
            even[line, 7:8, :] = value[7:]

    def store_scale(plane, cell, value):
        line, at = place_of(plane, cell)
        scale[line, at : at + 8, :] = value

    def near_copies(cycle, buffer, send_sems, recv_sems):
        copies = []
        for k in range(1, reach + 1):
            for sign in (1, -1):
                to = place(lax.rem(me + sign * k + everyone, everyone))
                slot = reach - sign * k
                copies.append(
                    send(
                        buffer.at[cycle, reach], buffer.at[cycle, slot],
                        send_sems.at[cycle, slot], recv_sems.at[cycle, slot], to,
                    )
                )
        return copies

    factors = []
    for orbital in range(count):
        taken = rank * count + orbital < counts[0]
        factors.append(
            jnp.where(taken, occupations[0, orbital], jnp.float32(0.0)) / (ranks * count)
        )
    norms = [jnp.float32(1.0)] * count
    h_copies = None

    for cycle in range(CYCLES):
        last = cycle + 1 == CYCLES
        if cycle == 0:
            loaded(ionic, load_sem.at[0])
            flat[...] = ionic[...]
        else:
            for tile in range(tiles):
                lanes = slice(tile * LANES, (tile + 1) * LANES)
                for group in range(0, box, 8):
                    first = group // planes
                    pieces = [box_pot[first + i, :, lanes] for i in range(8 // planes)]
                    flat[tile, group : group + 8, :] = ionic[
                        tile, group : group + 8, :
                    ] + jnp.concatenate(pieces, axis=0)
        potential = flat[...]
        lowest = jnp.min(jnp.min(potential, axis=0), axis=0, keepdims=True)
        lowest = jnp.min(lowest, axis=1, keepdims=True)
        highest = jnp.max(jnp.max(potential, axis=0), axis=0, keepdims=True)
        highest = jnp.max(highest, axis=1, keepdims=True)
        low_bound = lowest + CUTOFF
        high_bound = highest + 6.0
        center = 0.5 * (high_bound + low_bound)
        inverse = 1.0 / (0.5 * (high_bound - low_bound))
        flat[...] = (2.0 * inverse) * ((3.0 - center) + potential)
        shape.spread(lambda _, tile, plane: strided(flat, tile, plane), store_scale)
        if cycle == 0:
            for orbital in range(count):
                loaded(planes_of.at[orbital], load_sem.at[1 + orbital])
            shape.spread(
                lambda orbital, tile, plane: strided(planes_of.at[orbital], tile, plane),
                store_orbitals,
            )

        filter_step(shape, even, odd, scale, inverse, True)
        if cycle == 0:
            pl.semaphore_wait(barrier, everyone - 1)
            guess.wait()
            h_copies = near_copies(0, near_h, h_send, h_recv)
            for copy in h_copies:
                copy.start()

        def two_steps(step, carry):
            filter_step(shape, odd, even, scale, inverse, False)
            filter_step(shape, even, odd, scale, inverse, False)
            return carry

        lax.fori_loop(0, (DEGREE - 1) // 2, two_steps, 0)
        filter_step(shape, odd, even, scale, inverse, False)

        total = jnp.zeros((8, LANES), jnp.float32)
        for base in range(0, SIDE, 8):
            value = even[: shape.deep * shape.lines, 8 + base : 16 + base, :]
            total = total + jnp.sum(value * value, axis=0)
        shares = jnp.zeros((8, LANES), jnp.float32)
        for orbital in range(count):
            square = jnp.sum(
                jnp.where(orbital_of == orbital, total, 0.0), axis=0, keepdims=True
            )
            square = jnp.sum(square, axis=1, keepdims=True)
            square = norms[orbital] * square * (1.0 / (box * cells)) + 1e-06
            share = factors[orbital] * norms[orbital] / square
            shares = jnp.where(orbital_of == orbital, share, shares)
            norms[orbital] = norms[orbital] / square

        def load_density(plane, cell):
            line, at = place_of(plane, cell)
            value = even[line, 8 + at : 16 + at, :]
            return shares * (value * value)

        def store_density(plane, tile, value):
            flat[tile, pl.ds(plane, shape.across, stride=shape.deep), :] = value

        shape.gather(load_density, store_density)
        if cycle == 0:
            loaded(core, load_sem.at[2 + count])
        found = jnp.zeros((8, LANES), jnp.float32) if cycle == 0 else charge[...]
        for group in range(0, box, 8):
            rows = slice(group, group + 8)
            weight = weight_rows[rows, :]
            for tile in range(tiles):
                density = flat[tile, rows, :] + core[tile, rows, :] * (1.0 / ranks)
                density = density * weight
                found = found + density
                for piece in range(8 // planes):
                    weighted[
                        group // planes + piece, :, tile * LANES : (tile + 1) * LANES
                    ] = density[piece * planes : (piece + 1) * planes]
        charge[...] = found

        down = (lax.rem(dom + doms - 1, doms), rank)
        up = (lax.rem(dom + 1, doms), rank)
        rims = [
            send(
                weighted.at[:rim], rim_in.at[cycle, 1],
                rim_send.at[cycle, 1], rim_recv.at[cycle, 1], down,
            ),
            send(
                weighted.at[rim + ranks :], rim_in.at[cycle, 0],
                rim_send.at[cycle, 0], rim_recv.at[cycle, 0], up,
            ),
        ]
        for copy in rims:
            copy.start()

        def sum_copy(k):
            to = (dom, lax.rem(rank + k, ranks))
            return send(sums.at[rank], sums.at[rank], sum_send.at[k], sum_recv.at[rank], to)

        if last:
            sums[rank] = found
            repeat(1, ranks, lambda k: sum_copy(k).start())

        def part_copy(owner, cycle=cycle):
            return send(
                weighted.at[owner + rim], parts.at[cycle, rank],
                part_send.at[cycle, owner], part_recv.at[cycle, rank], (dom, owner),
            )

        def give(owner):
            @pl.when(owner != rank)
            def _():
                part_copy(owner).start()

        repeat(rim, ranks - rim, give)

        def join(step):
            side = lax.rem(dom + 1 + step, 2)
            arrived(rim_in.at[cycle, side], rim_recv.at[cycle, side])
            base = side * (ranks - rim)
            for j in range(rim):
                weighted[rim + base + j] += rim_in[cycle, side, j]
                give(base + j)

        repeat(0, 2, join)

        near_d[cycle, reach] = weighted[rank + rim]

        def take(k):
            slot = lax.rem(rank + k, ranks)
            arrived(parts.at[cycle, slot], part_recv.at[cycle, slot])
            near_d[cycle, reach] += parts[cycle, slot]

        repeat(1, ranks, take)
        d_copies = near_copies(cycle, near_d, d_send, d_recv)
        for copy in d_copies:
            copy.start()

        def dom_copy(k):
            to = (lax.rem(dom + k, doms), rank)
            return send(dom_sums.at[dom], dom_sums.at[dom], dom_send.at[k], dom_recv.at[dom], to)

        if last:
            def take_sum(k):
                slot = lax.rem(rank + k, ranks)
                arrived(sums.at[slot], sum_recv.at[slot])

            repeat(1, ranks, take_sum)
            dom_sums[dom] = jnp.sum(sums[...], axis=0)
            repeat(1, doms, lambda k: dom_copy(k).start())

        work[...] = jnp.zeros_like(work)
        work_d[...] = jnp.zeros_like(work_d)
        for slot in range(2 * reach + 1):
            if slot != reach:
                arrived(near_h.at[cycle, slot], h_recv.at[cycle, slot])
            work[slot * planes : (slot + 1) * planes, :] = near_h[cycle, slot]
        for slot in range(2 * reach + 1):
            if slot != reach:
                arrived(near_d.at[cycle, slot], d_recv.at[cycle, slot])
            work_d[slot * planes : (slot + 1) * planes, :] = near_d[cycle, slot]

        field = work[...]
        source = FOUR_PI * work_d[...]
        height = field.shape[0]
        column = lax.broadcasted_iota(jnp.int32, field.shape, 1) % SIDE
        for _ in range(SWEEPS):
            left = jnp.where(
                column == 0, pltpu.roll(field, cells - (SIDE - 1), 1), pltpu.roll(field, 1, 1)
            )
            right = jnp.where(
                column == SIDE - 1, pltpu.roll(field, SIDE - 1, 1),
                pltpu.roll(field, cells - 1, 1),
            )
            near = pltpu.roll(field, 1, 0) + pltpu.roll(field, height - 1, 0)
            near = near + left + right
            near = near + pltpu.roll(field, SIDE, 1) + pltpu.roll(field, cells - SIDE, 1)
            field = field + RELAXATION * ((near + source) * (1.0 / 6.0) - field)
        work[...] = field
        mine = work[reach * planes : (reach + 1) * planes, :]
        density = near_d[cycle, reach]
        root = jnp.exp(jnp.log(density) * (1.0 / 3.0))
        root = root - (root - density / (root * root)) * (1.0 / 3.0)
        result = mine - EXCHANGE_FACTOR * root

        for copy in h_copies:
            copy.wait_send()
        if not last:
            slot = rank + rim
            box_pot[slot] = result

            def box_copy(k):
                to = (dom, lax.rem(rank + k, ranks))
                return send(
                    box_pot.at[rank + rim], box_pot.at[rank + rim],
                    box_send.at[k], box_recv.at[rank + rim], to,
                )

            repeat(1, ranks, lambda k: box_copy(k).start())
            near_h[cycle + 1, reach] = mine
            h_copies = near_copies(cycle + 1, near_h, h_send, h_recv)
            for copy in h_copies:
                copy.start()

            def relay_copy(index):
                side, j = lax.div(index, rim), lax.rem(index, rim)
                owner = side * (ranks - rim) + j
                target = jnp.where(side == 0, chunks - rim + j, j)
                to_dom = lax.rem(dom + jnp.where(side == 0, doms - 1, 1), doms)
                return send(
                    box_pot.at[owner + rim], box_pot.at[target],
                    relay_send.at[index], box_recv.at[target], (to_dom, rank),
                )

            def relay(index):
                side, j = lax.div(index, rim), lax.rem(index, rim)
                owner = side * (ranks - rim) + j

                @pl.when(owner != rank)
                def _():
                    arrived(box_pot.at[owner + rim], box_recv.at[owner + rim])

                relay_copy(index).start()

            repeat(0, 2 * rim, relay)

            def take_core(owner):
                @pl.when(owner != rank)
                def _():
                    arrived(box_pot.at[owner + rim], box_recv.at[owner + rim])

            def take_rim(index):
                arrived(box_pot.at[index], box_recv.at[index])
                target = rim + ranks + index
                arrived(box_pot.at[target], box_recv.at[target])

            repeat(rim, ranks - rim, take_core)
            repeat(0, rim, take_rim)
            repeat(1, ranks, lambda k: box_copy(k).wait_send())
            repeat(0, 2 * rim, lambda index: relay_copy(index).wait_send())

        for copy in rims + d_copies:
            copy.wait_send()

        def gave(owner):
            @pl.when(owner != rank)
            def _():
                part_copy(owner).wait_send()

        repeat(0, ranks, gave)
        if last:
            def take_dom(k):
                slot = lax.rem(dom + k, doms)
                arrived(dom_sums.at[slot], dom_recv.at[slot])

            repeat(1, doms, take_dom)
            total = jnp.sum(jnp.sum(dom_sums[...], axis=0), axis=0, keepdims=True)
            total = jnp.sum(total, axis=1, keepdims=True)
            average = total / (everyone * planes * cells)
            shift = (-SWEEPS * RELAXATION * FOUR_PI / 6.0) * average
            output[...] = result + shift
            repeat(1, ranks, lambda k: sum_copy(k).wait_send())
            repeat(1, doms, lambda k: dom_copy(k).wait_send())


def body(
    orbitals, occupations, occupied_count, weights, external_potential, core_density, hartree_guess
):
    doms, ranks = lax.axis_size("dom"), lax.axis_size("orb")
    count, box, cells = orbitals.shape[1:]
    planes = hartree_guess.shape[0]
    chunks = box // planes
    rim = BUF // planes
    reach = -(-SWEEPS // planes)
    span = 2 * reach + 1
    rows = -(-span * planes // 8) * 8
    shape = Segments(count, box, cells)
    lines = shape.deep * shape.lines
    f32 = jnp.float32
    anywhere = pl.BlockSpec(memory_space=pl.ANY)
    scalars = pl.BlockSpec(memory_space=pltpu.SMEM)
    dma = pltpu.SemaphoreType.DMA
    vmem = lambda *dims: pltpu.VMEM(dims, f32)
    return pl.pallas_call(
        functools.partial(cycles_kernel, doms, ranks),
        out_shape=jax.ShapeDtypeStruct((planes, cells), f32),
        in_specs=[anywhere, scalars, scalars, scalars, anywhere, anywhere, anywhere],
        out_specs=pl.BlockSpec(memory_space=pltpu.VMEM),
        scratch_shapes=[
            vmem(count, shape.tiles, box, LANES),
            vmem(shape.tiles, box, LANES),
            vmem(shape.tiles, box, LANES),
            vmem(shape.tiles, box, LANES),
            vmem(box, LANES),
            vmem(lines, SIDE + 16, LANES),
            vmem(lines, SIDE + 16, LANES),
            vmem(lines, SIDE, LANES),
            vmem(8, LANES),
            vmem(chunks, planes, cells),
            vmem(CYCLES, 2, rim, planes, cells),
            vmem(CYCLES, ranks, planes, cells),
            vmem(CYCLES, span, planes, cells),
            vmem(CYCLES, span, planes, cells),
            vmem(rows, cells),
            vmem(rows, cells),
            vmem(chunks, planes, cells),
            vmem(ranks, 8, LANES),
            vmem(doms, 8, LANES),
            dma((3 + count,)),
            dma((CYCLES, 2)), dma((CYCLES, 2)),
            dma((CYCLES, ranks)), dma((CYCLES, ranks)),
            dma((CYCLES, span)), dma((CYCLES, span)),
            dma((CYCLES, span)), dma((CYCLES, span)),
            dma((ranks,)), dma((ranks,)),
            dma((doms,)), dma((doms,)),
            dma((ranks,)), dma((chunks,)),
            dma((2 * rim,)),
        ],
        compiler_params=pltpu.CompilerParams(collective_id=0, has_side_effects=True),
        name="cycles",
    )(
        orbitals[0], occupations, occupied_count, weights, external_potential[0],
        core_density[0], hartree_guess,
    )


def solution(mesh):
    placed = (
        P("dom", "orb", None, None),
        P("dom", "orb"),
        P("dom"),
        P("dom", None),
        P("dom", None, None),
        P("dom", None, None),
        P(("dom", "orb"), None),
    )
    return jax.shard_map(
        body, mesh=mesh, in_specs=placed, out_specs=P(("dom", "orb"), None), check_vma=False
    )
```

time: 91.9 us -> 60.9 us (0.66)
  Pallas kernels: 87 us -> 58.6 us
  local copies, waits for them, and re-layouts: 3.39 us -> 1.39 us
    pallas_call x2 -> x1, Pallas kernels: 87 us -> 58.6 us  [body(): pl.pallas_call(functools.partial(cycles_kernel, doms, ranks), out_shape=j...]
    unnamed x5 -> x1, local copies, waits for them, and re-layouts: 2.69 us -> 1.39 us
where the time goes in v1:
time: 60.9 us; the launch traced here: 60.6 us
  Pallas kernels  58.6 us (96%)
  local copies, waits for them, and re-layouts  1.39 us (2%)
  between operations  0.66 us (1%)
    pallas_call x1, Pallas kernels, body(): pl.pallas_call(functools.partial(cycles_kernel, doms, ranks), out_shape=j...  58.6 us
    unnamed x1, local copies, waits for them, and re-layouts  1.39 us

profile of v1, /device:TPU:0, one launch (start us, length us, event | category | flops | bytes accessed | tf_op | source)
XLA Modules:
  0.0 60.6 jit_solution(850630843861113203)
XLA Ops:
  0.7 58.6 %cycles.1 = f32[4,2304]{1,0:T(4,128)} custom-call(f32[2,48,2304]{2,1,0:T(8,128)} %bitcast.3, f32[1,2]{1,0:T(1,128)} %refs_1_.1, s32[1]{0:T(128)S(6)} %copy.9.refs_2_, f32[1,48]{1,0:T(1,128)} %refs_3_.1, f32[48,2304]{1,0:T(8,128)} %bitcast.4, f32[48,2304]{1,0:T(8,128)} %bitcast.5, f32[4,2304]{1,0:T(4,128)} %refs_6_.1), custom_call_target="tpu_custom_call" | custom-call | tf_op jit(solution)/shard_map/cycles/pallas_call | solution.py:566
  59.2 1.4 %copy.10 = f32[4,2304]{1,0:T(4,128)} copy(f32[4,2304]{1,0:T(4,128)} %cycles.1) | data formatting | bytes 73728

commit v2 on v1

--- a/solution.py
+++ b/solution.py
@@ -16,6 +16,8 @@
 HALF = 64
 SEGMENTS = 4
 GROUP = 4
+PITCH = 72
+SCALE_PITCH = 56
 
 
 EXCHANGE_FACTOR = (3.0 / 3.141592653589793) ** (1.0 / 3.0)
@@ -37,8 +39,12 @@
         self.tiles = cells // LANES
         self.blocks = -(-self.length // LANES)
         self.shift = count * self.across
+        self.stored = (self.deep + 2) * (self.lines + 2)
         assert self.deep * self.across == box and self.length % HALF == 0
         assert self.tiles * LANES == cells and SIDE % 8 == 0 and box % 8 == 0
+
+    def block(self, plane, line):
+        return (plane + 1) * (self.lines + 2) + line + 1
 
     def spread(self, load, store):
         lane = lax.broadcasted_iota(jnp.int32, (self.across, LANES), 1)
@@ -102,65 +108,72 @@
                 store(plane, tile, low if low is high else jnp.where(lane < HALF, low, high))
 
 
+def put_cells(shape, target, plane, start, base, value):
+    block = slice(shape.block(plane, start), shape.block(plane, start) + value.shape[0])
+    target[block, 8 + base : 16 + base, :] = value
+    if base == 0:
+        target[block, 8 + SIDE : 9 + SIDE, :] = value[:, :1, :]
+    if base == SIDE - 8:
+        target[block, 7:8, :] = value[:, 7:, :]
+
+
+def put_faces(shape, target, plane, start, base, value):
+    lines, deep, across = shape.lines, shape.deep, shape.across
+    count = value.shape[0]
+    cells = slice(8 + base, 16 + base)
+
+    def turn(part, amount):
+        return pltpu.roll(part.reshape(-1, LANES), amount, 1).reshape(part.shape)
+
+    def at(plane, line, number):
+        first = shape.block(plane, line)
+        return slice(first, first + number)
+
+    lane = lax.broadcasted_iota(jnp.int32, value.shape, 2) % across
+    if plane == deep - 1:
+        target[at(-1, start, count), cells, :] = jnp.where(lane != 0, turn(value, 1), 0.0)
+    if plane == 0:
+        target[at(deep, start, count), cells, :] = jnp.where(
+            lane != across - 1, turn(value, LANES - 1), 0.0
+        )
+    if start == 0:
+        target[at(plane, lines, 1), cells, :] = turn(value[:1], LANES - shape.shift)
+    if start + count == lines:
+        target[at(plane, -1, 1), cells, :] = turn(value[count - 1 :], shape.shift)
+
+
 def filter_step(shape, source, target, scale, inverse, first):
-    lines, deep, across = shape.lines, shape.deep, shape.across
-    lane = lax.broadcasted_iota(jnp.int32, (1, 8, LANES), 2) % across
-    has_left = jnp.broadcast_to(lane != 0, (GROUP, 8, LANES))
-    has_right = jnp.broadcast_to(lane != across - 1, (GROUP, 8, LANES))
-
-    def turn(value, amount):
-        return pltpu.roll(value.reshape(-1, LANES), amount, 1).reshape(value.shape)
-
+    lines, deep = shape.lines, shape.deep
     for base in range(0, SIDE, 8):
         cells = slice(8 + base, 16 + base)
-
-        def line(plane, at):
-            return source[plane * lines + at : plane * lines + at + 1, cells, :]
-
         for start in range(0, lines, GROUP):
-            middles = [
-                source[plane * lines + start : plane * lines + start + GROUP, cells, :]
-                for plane in range(deep)
+            grown = [
+                source[shape.block(plane, start - 1) : shape.block(plane, start + GROUP + 1), cells, :]
+                if 0 <= plane < deep
+                else source[shape.block(plane, start) : shape.block(plane, start + GROUP), cells, :]
+                for plane in range(-1, deep + 1)
             ]
+            middles = [part[1:-1] if 0 < i <= deep else part for i, part in enumerate(grown)]
             for plane in range(deep):
-                block = slice(plane * lines + start, plane * lines + start + GROUP)
-                middle = middles[plane]
-                if plane > 0:
-                    left = middles[plane - 1]
-                else:
-                    left = jnp.where(has_left, turn(middles[deep - 1], 1), 0.0)
-                if plane < deep - 1:
-                    right = middles[plane + 1]
-                else:
-                    right = jnp.where(has_right, turn(middles[0], LANES - 1), 0.0)
-                if start > 0:
-                    below = line(plane, start - 1)
-                else:
-                    below = turn(line(plane, lines - 1), shape.shift)
-                if start + GROUP < lines:
-                    above = line(plane, start + GROUP)
-                else:
-                    above = turn(line(plane, 0), LANES - shape.shift)
-                below = jnp.concatenate([below, middle[:-1]], axis=0)
-                above = jnp.concatenate([middle[1:], above], axis=0)
+                first_block = shape.block(plane, start)
+                block = slice(first_block, first_block + GROUP)
+                rows = slice(plane * lines + start, plane * lines + start + GROUP)
+                middle = middles[plane + 1]
                 near = source[block, 7 + base : 15 + base, :] + source[block, 9 + base : 17 + base, :]
-                near = near + (below + above)
-                near = near + (left + right)
-                value = scale[block, base : base + 8, :] * middle - inverse * near
+                near = near + (grown[plane + 1][:-2] + grown[plane + 1][2:])
+                near = near + (middles[plane] + middles[plane + 2])
+                value = scale[rows, base : base + 8, :] * middle - inverse * near
                 if first:
                     value = 0.5 * value
                 else:
                     value = value - target[block, cells, :]
-                target[block, cells, :] = value
-                if base == 0:
-                    target[block, 8 + SIDE : 9 + SIDE, :] = value[:, :1, :]
-                if base == SIDE - 8:
-                    target[block, 7:8, :] = value[:, 7:, :]
+                put_cells(shape, target, plane, start, base, value)
+                put_faces(shape, target, plane, start, base, value)
 
 
 def cycles_kernel(doms, ranks, *refs):
     (
-        orbitals_hbm, occupations, counts, weights, ionic_hbm, core_hbm, hartree_hbm,
+        orbitals_hbm, occupations, occupied, weights, ionic_hbm, core_hbm, hartree_hbm,
         output,
         planes_of, ionic, core, flat, weight_rows, even, odd, scale, charge,
         weighted, rim_in, parts, near_h, near_d, work, work_d, box_pot, sums, dom_sums,
@@ -172,7 +185,9 @@
     shape = Segments(count, box, cells)
     tiles = shape.tiles
     rim = BUF // planes
-    reach = near_h.shape[1] // 2
+    span = near_h.shape[1]
+    reach = span // 2
+    assert planes + 2 * (SWEEPS - 2) <= 8
     everyone = doms * ranks
     dom = lax.axis_index("dom")
     rank = lax.axis_index("orb")
@@ -189,6 +204,13 @@
 
     def repeat(low, high, step):
         lax.fori_loop(low, high, lambda i, carry: (step(i), carry)[1], 0)
+
+    def outward(low, high, step):
+        def both(i):
+            pl.when(ranks - 1 - i > rank)(lambda: step(ranks - 1 - i))
+            pl.when(i < rank)(lambda: step(i))
+
+        repeat(low, high, both)
 
     def arrived(target, sem):
         send(target, target, sem, sem, (dom, rank)).wait_recv()
@@ -233,20 +255,11 @@
     def strided(ref, tile, plane):
         return ref[tile, pl.ds(plane, shape.across, stride=shape.deep), :]
 
-    def place_of(plane, cell):
-        return plane * shape.lines + cell // SIDE, cell % SIDE
-
     def store_orbitals(plane, cell, value):
-        line, at = place_of(plane, cell)
-        even[line, 8 + at : 16 + at, :] = value
-        if at == 0:
-            even[line, 8 + SIDE : 9 + SIDE, :] = value[:1]
-        if at == SIDE - 8:
-            even[line, 7:8, :] = value[7:]
+        put_cells(shape, even, plane, cell // SIDE, cell % SIDE, value[None])
 
     def store_scale(plane, cell, value):
-        line, at = place_of(plane, cell)
-        scale[line, at : at + 8, :] = value
+        scale[plane * shape.lines + cell // SIDE, cell % SIDE : cell % SIDE + 8, :] = value
 
     def near_copies(cycle, buffer, send_sems, recv_sems):
         copies = []
@@ -264,7 +277,7 @@
 
     factors = []
     for orbital in range(count):
-        taken = rank * count + orbital < counts[0]
+        taken = rank * count + orbital < occupied[0, 0]
         factors.append(
             jnp.where(taken, occupations[0, orbital], jnp.float32(0.0)) / (ranks * count)
         )
@@ -303,6 +316,12 @@
                 lambda orbital, tile, plane: strided(planes_of.at[orbital], tile, plane),
                 store_orbitals,
             )
+            for base in range(0, SIDE, 8):
+                for start in range(0, shape.lines, GROUP):
+                    for plane in range(shape.deep):
+                        first = shape.block(plane, start)
+                        value = even[first : first + GROUP, 8 + base : 16 + base, :]
+                        put_faces(shape, even, plane, start, base, value)
 
         filter_step(shape, even, odd, scale, inverse, True)
         if cycle == 0:
@@ -322,8 +341,11 @@
 
         total = jnp.zeros((8, LANES), jnp.float32)
         for base in range(0, SIDE, 8):
-            value = even[: shape.deep * shape.lines, 8 + base : 16 + base, :]
-            total = total + jnp.sum(value * value, axis=0)
+            for plane in range(shape.deep):
+                value = even[
+                    shape.block(plane, 0) : shape.block(plane, shape.lines), 8 + base : 16 + base, :
+                ]
+                total = total + jnp.sum(value * value, axis=0)
         shares = jnp.zeros((8, LANES), jnp.float32)
         for orbital in range(count):
             square = jnp.sum(
@@ -336,8 +358,8 @@
             norms[orbital] = norms[orbital] / square
 
         def load_density(plane, cell):
-            line, at = place_of(plane, cell)
-            value = even[line, 8 + at : 16 + at, :]
+            at = cell % SIDE
+            value = even[shape.block(plane, cell // SIDE), 8 + at : 16 + at, :]
             return shares * (value * value)
 
         def store_density(plane, tile, value):
@@ -390,11 +412,9 @@
             )
 
         def give(owner):
-            @pl.when(owner != rank)
-            def _():
-                part_copy(owner).start()
-
-        repeat(rim, ranks - rim, give)
+            part_copy(owner).start()
+
+        outward(rim, ranks - rim, give)
 
         def join(step):
             side = lax.rem(dom + 1 + step, 2)
@@ -402,7 +422,7 @@
             base = side * (ranks - rim)
             for j in range(rim):
                 weighted[rim + base + j] += rim_in[cycle, side, j]
-                give(base + j)
+                pl.when(base + j != rank)(lambda: give(base + j))
 
         repeat(0, 2, join)
 
@@ -431,22 +451,34 @@
             dom_sums[dom] = jnp.sum(sums[...], axis=0)
             repeat(1, doms, lambda k: dom_copy(k).start())
 
-        work[...] = jnp.zeros_like(work)
-        work_d[...] = jnp.zeros_like(work_d)
-        for slot in range(2 * reach + 1):
+        height = work.shape[0]
+        origin = reach * planes - 2
+
+        def put(target, slot, value):
+            run = min(planes, 2)
+            for row in range(0, planes, run):
+                at = (slot * planes + row - origin) % height
+                target[at : at + run, :] = value[row : row + run]
+
+        if span * planes < height:
+            work[...] = jnp.zeros_like(work)
+            work_d[...] = jnp.zeros_like(work_d)
+        for slot in range(span):
             if slot != reach:
                 arrived(near_h.at[cycle, slot], h_recv.at[cycle, slot])
-            work[slot * planes : (slot + 1) * planes, :] = near_h[cycle, slot]
-        for slot in range(2 * reach + 1):
+            put(work, slot, near_h[cycle, slot])
+        for slot in range(span):
             if slot != reach:
                 arrived(near_d.at[cycle, slot], d_recv.at[cycle, slot])
-            work_d[slot * planes : (slot + 1) * planes, :] = near_d[cycle, slot]
+            put(work_d, slot, near_d[cycle, slot])
 
         field = work[...]
         source = FOUR_PI * work_d[...]
-        height = field.shape[0]
         column = lax.broadcasted_iota(jnp.int32, field.shape, 1) % SIDE
-        for _ in range(SWEEPS):
+        for sweep in range(SWEEPS):
+            near = pltpu.roll(field, 1, 0) + pltpu.roll(field, field.shape[0] - 1, 0)
+            if sweep == 1:
+                field, near, source, column = field[:8], near[:8], source[:8], column[:8]
             left = jnp.where(
                 column == 0, pltpu.roll(field, cells - (SIDE - 1), 1), pltpu.roll(field, 1, 1)
             )
@@ -454,12 +486,11 @@
                 column == SIDE - 1, pltpu.roll(field, SIDE - 1, 1),
                 pltpu.roll(field, cells - 1, 1),
             )
-            near = pltpu.roll(field, 1, 0) + pltpu.roll(field, height - 1, 0)
             near = near + left + right
             near = near + pltpu.roll(field, SIDE, 1) + pltpu.roll(field, cells - SIDE, 1)
             field = field + RELAXATION * ((near + source) * (1.0 / 6.0) - field)
-        work[...] = field
-        mine = work[reach * planes : (reach + 1) * planes, :]
+        work[:8, :] = field
+        mine = work[2 : 2 + planes, :]
         density = near_d[cycle, reach]
         root = jnp.exp(jnp.log(density) * (1.0 / 3.0))
         root = root - (root - density / (root * root)) * (1.0 / 3.0)
@@ -471,14 +502,13 @@
             slot = rank + rim
             box_pot[slot] = result
 
-            def box_copy(k):
-                to = (dom, lax.rem(rank + k, ranks))
+            def box_copy(to):
                 return send(
                     box_pot.at[rank + rim], box_pot.at[rank + rim],
-                    box_send.at[k], box_recv.at[rank + rim], to,
+                    box_send.at[to], box_recv.at[rank + rim], (dom, to),
                 )
 
-            repeat(1, ranks, lambda k: box_copy(k).start())
+            outward(0, ranks, lambda to: box_copy(to).start())
             near_h[cycle + 1, reach] = mine
             h_copies = near_copies(cycle + 1, near_h, h_send, h_recv)
             for copy in h_copies:
@@ -494,7 +524,8 @@
                     relay_send.at[index], box_recv.at[target], (to_dom, rank),
                 )
 
-            def relay(index):
+            def relay(step):
+                index = lax.rem(step + jnp.where(2 * rank < ranks, 0, rim), 2 * rim)
                 side, j = lax.div(index, rim), lax.rem(index, rim)
                 owner = side * (ranks - rim) + j
 
@@ -518,18 +549,13 @@
 
             repeat(rim, ranks - rim, take_core)
             repeat(0, rim, take_rim)
-            repeat(1, ranks, lambda k: box_copy(k).wait_send())
+            outward(0, ranks, lambda to: box_copy(to).wait_send())
             repeat(0, 2 * rim, lambda index: relay_copy(index).wait_send())
 
         for copy in rims + d_copies:
             copy.wait_send()
 
-        def gave(owner):
-            @pl.when(owner != rank)
-            def _():
-                part_copy(owner).wait_send()
-
-        repeat(0, ranks, gave)
+        outward(0, ranks, lambda owner: part_copy(owner).wait_send())
         if last:
             def take_dom(k):
                 slot = lax.rem(dom + k, doms)
@@ -565,7 +591,7 @@
     vmem = lambda *dims: pltpu.VMEM(dims, f32)
     return pl.pallas_call(
         functools.partial(cycles_kernel, doms, ranks),
-        out_shape=jax.ShapeDtypeStruct((planes, cells), f32),
+        out_shape=pltpu.VMEM((planes, cells), f32),
         in_specs=[anywhere, scalars, scalars, scalars, anywhere, anywhere, anywhere],
         out_specs=pl.BlockSpec(memory_space=pltpu.VMEM),
         scratch_shapes=[
@@ -574,9 +600,9 @@
             vmem(shape.tiles, box, LANES),
             vmem(shape.tiles, box, LANES),
             vmem(box, LANES),
-            vmem(lines, SIDE + 16, LANES),
-            vmem(lines, SIDE + 16, LANES),
-            vmem(lines, SIDE, LANES),
+            vmem(shape.stored, PITCH, LANES),
+            vmem(shape.stored, PITCH, LANES),
+            vmem(lines, SCALE_PITCH, LANES),
             vmem(8, LANES),
             vmem(chunks, planes, cells),
             vmem(CYCLES, 2, rim, planes, cells),
@@ -601,7 +627,7 @@
         compiler_params=pltpu.CompilerParams(collective_id=0, has_side_effects=True),
         name="cycles",
     )(
-        orbitals[0], occupations, occupied_count, weights, external_potential[0],
+        orbitals[0], occupations, occupied_count.reshape(1, 1), weights, external_potential[0],
         core_density[0], hartree_guess,
     )
 

time: 60.9 us -> 54.9 us (0.901)
  Pallas kernels: 58.6 us -> 53.4 us
  local copies, waits for them, and re-layouts: 1.39 us -> 0.62 us
    pallas_call x1, Pallas kernels: 58.6 us -> 53.4 us  [body(): pl.pallas_call(functools.partial(cycles_kernel, doms, ranks), out_shape=p...]
    unnamed x1, local copies, waits for them, and re-layouts: 1.39 us -> 0.62 us
where the time goes in v2:
time: 54.9 us; the launch traced here: 54.7 us
  Pallas kernels  53.4 us (97%)
  between operations  0.66 us (1%)
  local copies, waits for them, and re-layouts  0.62 us (1%)
    pallas_call x1, Pallas kernels, body(): pl.pallas_call(functools.partial(cycles_kernel, doms, ranks), out_shape=p...  53.4 us

profile of v2, /device:TPU:0, one launch (start us, length us, event | category | flops | bytes accessed | tf_op | source)
XLA Modules:
  0.0 54.7 jit_solution(3210537119018229240)
XLA Ops:
  0.7 53.4 %cycles.1 = f32[4,2304]{1,0:T(4,128)S(1)} custom-call(f32[2,48,2304]{2,1,0:T(8,128)} %bitcast.5, f32[1,2]{1,0:T(1,128)} %refs_1_.1, s32[1,1]{1,0:T(1,128)} %bitcast.4.refs_2_, f32[1,48]{1,0:T(1,128)} %refs_3_.1, f32[48,2304]{1,0:T(8,128)} %bitcast.6, f32[48,2304]{1,0:T(8,128)} %bitcast.7, f32[4,2304]{1,0:T(4,128)} %refs_6_.1), custom_call_target="tpu_custom_call" | custom-call | tf_op jit(solution)/shard_map/cycles/pallas_call | solution.py:592
  54.1 0.6 %copy.9 = f32[4,2304]{1,0:T(4,128)} copy(f32[4,2304]{1,0:T(4,128)S(1)} %cycles.1) | data formatting | bytes 73728

commit v3 on v2

--- a/solution.py
+++ b/solution.py
@@ -176,7 +176,7 @@
         orbitals_hbm, occupations, occupied, weights, ionic_hbm, core_hbm, hartree_hbm,
         output,
         planes_of, ionic, core, flat, weight_rows, even, odd, scale, charge,
-        weighted, rim_in, parts, near_h, near_d, work, work_d, box_pot, sums, dom_sums,
+        weighted, rim_in, parts, near_h, near_d, work, relaxed, grown, local, box_pot, sums, dom_sums,
         load_sem, rim_send, rim_recv, part_send, part_recv, h_send, h_recv, d_send, d_recv,
         sum_send, sum_recv, dom_send, dom_recv, box_send, box_recv, relay_send,
     ) = refs
@@ -215,6 +215,9 @@
     def arrived(target, sem):
         send(target, target, sem, sem, (dom, rank)).wait_recv()
 
+    def left(source, sem):
+        send(source, source, sem, sem, (dom, rank)).wait_send()
+
     def loads(source, target, sem):
         for tile in range(tiles):
             pltpu.make_async_copy(
@@ -228,10 +231,10 @@
 
     loads(ionic_hbm, ionic, load_sem.at[0])
     for orbital in range(count):
-        loads(orbitals_hbm.at[orbital], planes_of.at[orbital], load_sem.at[1 + orbital])
-    guess = pltpu.make_async_copy(hartree_hbm, near_h.at[0, reach], load_sem.at[1 + count])
+        loads(orbitals_hbm.at[orbital], planes_of.at[orbital], load_sem.at[1])
+    guess = pltpu.make_async_copy(hartree_hbm, near_h.at[0, reach], load_sem.at[2])
     guess.start()
-    loads(core_hbm, core, load_sem.at[2 + count])
+    loads(core_hbm, core, load_sem.at[3])
 
     barrier = pltpu.get_barrier_semaphore()
 
@@ -270,7 +273,7 @@
                 copies.append(
                     send(
                         buffer.at[cycle, reach], buffer.at[cycle, slot],
-                        send_sems.at[cycle, slot], recv_sems.at[cycle, slot], to,
+                        send_sems.at[cycle], recv_sems.at[cycle], to,
                     )
                 )
         return copies
@@ -282,6 +285,39 @@
             jnp.where(taken, occupations[0, orbital], jnp.float32(0.0)) / (ranks * count)
         )
     norms = [jnp.float32(1.0)] * count
+    height = work.shape[0]
+    origin = reach * planes - 2
+
+    def put(target, slot, value):
+        run = min(planes, 2)
+        for row in range(0, planes, run):
+            at = (slot * planes + row - origin) % height
+            target[at : at + run, :] = value[row : row + run]
+
+    def relax(field, added):
+        for sweep in range(SWEEPS):
+            if field is None:
+                field = added
+                continue
+            near = pltpu.roll(field, 1, 0) + pltpu.roll(field, field.shape[0] - 1, 0)
+            if sweep == 1:
+                field, near = field[:8], near[:8]
+            column = lax.broadcasted_iota(jnp.int32, field.shape, 1) % SIDE
+            left = jnp.where(
+                column == 0, pltpu.roll(field, cells - (SIDE - 1), 1), pltpu.roll(field, 1, 1)
+            )
+            right = jnp.where(
+                column == SIDE - 1, pltpu.roll(field, SIDE - 1, 1),
+                pltpu.roll(field, cells - 1, 1),
+            )
+            near = near + left + right
+            near = near + pltpu.roll(field, SIDE, 1) + pltpu.roll(field, cells - SIDE, 1)
+            field = field + RELAXATION * (near * (1.0 / 6.0) - field)
+            if added is not None:
+                field = field + added[: field.shape[0]]
+        return field
+
+    work[...] = jnp.zeros_like(work)
     h_copies = None
 
     for cycle in range(CYCLES):
@@ -310,8 +346,7 @@
         flat[...] = (2.0 * inverse) * ((3.0 - center) + potential)
         shape.spread(lambda _, tile, plane: strided(flat, tile, plane), store_scale)
         if cycle == 0:
-            for orbital in range(count):
-                loaded(planes_of.at[orbital], load_sem.at[1 + orbital])
+            loaded(planes_of, load_sem.at[1])
             shape.spread(
                 lambda orbital, tile, plane: strided(planes_of.at[orbital], tile, plane),
                 store_orbitals,
@@ -367,54 +402,61 @@
 
         shape.gather(load_density, store_density)
         if cycle == 0:
-            loaded(core, load_sem.at[2 + count])
+            loaded(core, load_sem.at[3])
+        def weigh(groups, found):
+            for group in groups:
+                rows = slice(group, group + 8)
+                weight = weight_rows[rows, :]
+                for tile in range(tiles):
+                    density = flat[tile, rows, :] + core[tile, rows, :] * (1.0 / ranks)
+                    density = density * weight
+                    found = found + density
+                    for piece in range(8 // planes):
+                        weighted[
+                            group // planes + piece, :, tile * LANES : (tile + 1) * LANES
+                        ] = density[piece * planes : (piece + 1) * planes]
+            return found
+
+        outer = list(range(0, BUF, 8)) + list(range(box - BUF, box, 8))
+        edges = list(range(BUF, 2 * BUF, 8)) + list(range(box - 2 * BUF, box - BUF, 8))
         found = jnp.zeros((8, LANES), jnp.float32) if cycle == 0 else charge[...]
-        for group in range(0, box, 8):
-            rows = slice(group, group + 8)
-            weight = weight_rows[rows, :]
-            for tile in range(tiles):
-                density = flat[tile, rows, :] + core[tile, rows, :] * (1.0 / ranks)
-                density = density * weight
-                found = found + density
-                for piece in range(8 // planes):
-                    weighted[
-                        group // planes + piece, :, tile * LANES : (tile + 1) * LANES
-                    ] = density[piece * planes : (piece + 1) * planes]
-        charge[...] = found
-
+        found = weigh(outer, found)
         down = (lax.rem(dom + doms - 1, doms), rank)
         up = (lax.rem(dom + 1, doms), rank)
         rims = [
             send(
                 weighted.at[:rim], rim_in.at[cycle, 1],
-                rim_send.at[cycle, 1], rim_recv.at[cycle, 1], down,
+                rim_send.at[cycle], rim_recv.at[cycle, 1], down,
             ),
             send(
                 weighted.at[rim + ranks :], rim_in.at[cycle, 0],
-                rim_send.at[cycle, 0], rim_recv.at[cycle, 0], up,
+                rim_send.at[cycle], rim_recv.at[cycle, 0], up,
             ),
         ]
         for copy in rims:
             copy.start()
+        found = weigh([g for g in range(2 * BUF, box - 2 * BUF, 8)], found)
 
         def sum_copy(k):
             to = (dom, lax.rem(rank + k, ranks))
-            return send(sums.at[rank], sums.at[rank], sum_send.at[k], sum_recv.at[rank], to)
-
+            return send(sums.at[rank], sums.at[rank], sum_send.at[0], sum_recv.at[0], to)
+
+        def part_copy(owner, cycle=cycle):
+            return send(
+                weighted.at[owner + rim], parts.at[cycle, rank],
+                part_send.at[cycle], part_recv.at[cycle], (dom, owner),
+            )
+
+        def give(owner):
+            part_copy(owner).start()
+
+        outward(rim, ranks - rim, give)
+        found = weigh(edges, found)
         if last:
             sums[rank] = found
             repeat(1, ranks, lambda k: sum_copy(k).start())
-
-        def part_copy(owner, cycle=cycle):
-            return send(
-                weighted.at[owner + rim], parts.at[cycle, rank],
-                part_send.at[cycle, owner], part_recv.at[cycle, rank], (dom, owner),
-            )
-
-        def give(owner):
-            part_copy(owner).start()
-
-        outward(rim, ranks - rim, give)
+        else:
+            charge[...] = found
 
         def join(step):
             side = lax.rem(dom + 1 + step, 2)
@@ -426,90 +468,63 @@
 
         repeat(0, 2, join)
 
-        near_d[cycle, reach] = weighted[rank + rim]
-
-        def take(k):
-            slot = lax.rem(rank + k, ranks)
-            arrived(parts.at[cycle, slot], part_recv.at[cycle, slot])
-            near_d[cycle, reach] += parts[cycle, slot]
-
-        repeat(1, ranks, take)
+        arrived(near_h.at[cycle, : span - 1], h_recv.at[cycle])
+        for slot in range(span):
+            put(work, slot, near_h[cycle, slot])
+        relaxed[...] = relax(work[...], None)
+
+        def dom_copy(k):
+            to = (lax.rem(dom + k, doms), rank)
+            return send(dom_sums.at[dom], dom_sums.at[dom], dom_send.at[0], dom_recv.at[0], to)
+
+        arrived(parts.at[cycle, : ranks - 1], part_recv.at[cycle])
+        density = weighted[rank + rim]
+        for k in range(1, ranks):
+            density = density + parts[cycle, lax.rem(rank + k, ranks)]
+        near_d[cycle, reach] = density
         d_copies = near_copies(cycle, near_d, d_send, d_recv)
         for copy in d_copies:
             copy.start()
 
-        def dom_copy(k):
-            to = (lax.rem(dom + k, doms), rank)
-            return send(dom_sums.at[dom], dom_sums.at[dom], dom_send.at[k], dom_recv.at[dom], to)
-
         if last:
-            def take_sum(k):
-                slot = lax.rem(rank + k, ranks)
-                arrived(sums.at[slot], sum_recv.at[slot])
-
-            repeat(1, ranks, take_sum)
+            arrived(sums.at[: ranks - 1], sum_recv.at[0])
             dom_sums[dom] = jnp.sum(sums[...], axis=0)
             repeat(1, doms, lambda k: dom_copy(k).start())
 
-        height = work.shape[0]
-        origin = reach * planes - 2
-
-        def put(target, slot, value):
-            run = min(planes, 2)
-            for row in range(0, planes, run):
-                at = (slot * planes + row - origin) % height
-                target[at : at + run, :] = value[row : row + run]
-
-        if span * planes < height:
-            work[...] = jnp.zeros_like(work)
-            work_d[...] = jnp.zeros_like(work_d)
-        for slot in range(span):
-            if slot != reach:
-                arrived(near_h.at[cycle, slot], h_recv.at[cycle, slot])
-            put(work, slot, near_h[cycle, slot])
-        for slot in range(span):
-            if slot != reach:
-                arrived(near_d.at[cycle, slot], d_recv.at[cycle, slot])
-            put(work_d, slot, near_d[cycle, slot])
-
-        field = work[...]
-        source = FOUR_PI * work_d[...]
-        column = lax.broadcasted_iota(jnp.int32, field.shape, 1) % SIDE
-        for sweep in range(SWEEPS):
-            near = pltpu.roll(field, 1, 0) + pltpu.roll(field, field.shape[0] - 1, 0)
-            if sweep == 1:
-                field, near, source, column = field[:8], near[:8], source[:8], column[:8]
-            left = jnp.where(
-                column == 0, pltpu.roll(field, cells - (SIDE - 1), 1), pltpu.roll(field, 1, 1)
-            )
-            right = jnp.where(
-                column == SIDE - 1, pltpu.roll(field, SIDE - 1, 1),
-                pltpu.roll(field, cells - 1, 1),
-            )
-            near = near + left + right
-            near = near + pltpu.roll(field, SIDE, 1) + pltpu.roll(field, cells - SIDE, 1)
-            field = field + RELAXATION * ((near + source) * (1.0 / 6.0) - field)
-        work[:8, :] = field
-        mine = work[2 : 2 + planes, :]
-        density = near_d[cycle, reach]
         root = jnp.exp(jnp.log(density) * (1.0 / 3.0))
         root = root - (root - density / (root * root)) * (1.0 / 3.0)
-        result = mine - EXCHANGE_FACTOR * root
-
-        for copy in h_copies:
-            copy.wait_send()
+        local[...] = relaxed[2 : 2 + planes, :] - EXCHANGE_FACTOR * root
+        arrived(near_d.at[cycle, : span - 1], d_recv.at[cycle])
+        for slot in range(span):
+            put(work, slot, near_d[cycle, slot])
+        if last:
+            arrived(dom_sums.at[: doms - 1], dom_recv.at[0])
+            total = jnp.sum(jnp.sum(dom_sums[...], axis=0), axis=0, keepdims=True)
+            total = jnp.sum(total, axis=1, keepdims=True)
+            average = total / (everyone * planes * cells)
+            shift = (-SWEEPS * RELAXATION * FOUR_PI / 6.0) * average
+            local[...] += shift
+        change = relax(None, (RELAXATION * FOUR_PI / 6.0) * work[...])
+        grown[...] = change
+        change = grown[2 : 2 + planes, :]
+        result = local[...] + change
+
+        left(near_h.at[cycle, : span - 1], h_send.at[cycle])
         if not last:
             slot = rank + rim
             box_pot[slot] = result
 
+            late = jnp.where(rank >= ranks - rim, rank - (ranks - 2 * rim), 2 * rim)
+            box_sem = jnp.where(rank < rim, rank, late)
+
             def box_copy(to):
                 return send(
                     box_pot.at[rank + rim], box_pot.at[rank + rim],
-                    box_send.at[to], box_recv.at[rank + rim], (dom, to),
+                    box_send.at[0], box_recv.at[box_sem], (dom, to),
                 )
 
             outward(0, ranks, lambda to: box_copy(to).start())
-            near_h[cycle + 1, reach] = mine
+            near_h[cycle + 1, reach] = relaxed[2 : 2 + planes, :] + change
             h_copies = near_copies(cycle + 1, near_h, h_send, h_recv)
             for copy in h_copies:
                 copy.start()
@@ -521,54 +536,41 @@
                 to_dom = lax.rem(dom + jnp.where(side == 0, doms - 1, 1), doms)
                 return send(
                     box_pot.at[owner + rim], box_pot.at[target],
-                    relay_send.at[index], box_recv.at[target], (to_dom, rank),
+                    relay_send.at[0], box_recv.at[2 * rim], (to_dom, rank),
                 )
 
             def relay(step):
-                index = lax.rem(step + jnp.where(2 * rank < ranks, 0, rim), 2 * rim)
+                index = lax.rem(step + rim * lax.rem(dom + 1, 2), 2 * rim)
                 side, j = lax.div(index, rim), lax.rem(index, rim)
                 owner = side * (ranks - rim) + j
 
                 @pl.when(owner != rank)
                 def _():
-                    arrived(box_pot.at[owner + rim], box_recv.at[owner + rim])
+                    arrived(box_pot.at[owner + rim], box_recv.at[index])
 
                 relay_copy(index).start()
 
             repeat(0, 2 * rim, relay)
-
-            def take_core(owner):
-                @pl.when(owner != rank)
-                def _():
-                    arrived(box_pot.at[owner + rim], box_recv.at[owner + rim])
-
-            def take_rim(index):
-                arrived(box_pot.at[index], box_recv.at[index])
-                target = rim + ranks + index
-                arrived(box_pot.at[target], box_recv.at[target])
-
-            repeat(rim, ranks - rim, take_core)
-            repeat(0, rim, take_rim)
-            outward(0, ranks, lambda to: box_copy(to).wait_send())
-            repeat(0, 2 * rim, lambda index: relay_copy(index).wait_send())
-
-        for copy in rims + d_copies:
-            copy.wait_send()
-
-        outward(0, ranks, lambda owner: part_copy(owner).wait_send())
+            at_edge = box_sem < 2 * rim
+
+            @pl.when(at_edge)
+            def _():
+                arrived(box_pot.at[:ranks], box_recv.at[2 * rim])
+
+            @pl.when(jnp.logical_not(at_edge))
+            def _():
+                arrived(box_pot.at[: ranks - 1], box_recv.at[2 * rim])
+
+            left(box_pot.at[: ranks - 1], box_send.at[0])
+            left(box_pot.at[: 2 * rim], relay_send.at[0])
+
+        left(rim_in.at[cycle], rim_send.at[cycle])
+        left(near_d.at[cycle, : span - 1], d_send.at[cycle])
+        left(parts.at[cycle, : ranks - 1], part_send.at[cycle])
         if last:
-            def take_dom(k):
-                slot = lax.rem(dom + k, doms)
-                arrived(dom_sums.at[slot], dom_recv.at[slot])
-
-            repeat(1, doms, take_dom)
-            total = jnp.sum(jnp.sum(dom_sums[...], axis=0), axis=0, keepdims=True)
-            total = jnp.sum(total, axis=1, keepdims=True)
-            average = total / (everyone * planes * cells)
-            shift = (-SWEEPS * RELAXATION * FOUR_PI / 6.0) * average
-            output[...] = result + shift
-            repeat(1, ranks, lambda k: sum_copy(k).wait_send())
-            repeat(1, doms, lambda k: dom_copy(k).wait_send())
+            output[...] = result
+            left(sums.at[: ranks - 1], sum_send.at[0])
+            left(dom_sums.at[: doms - 1], dom_send.at[0])
 
 
 def body(
@@ -610,19 +612,21 @@
             vmem(CYCLES, span, planes, cells),
             vmem(CYCLES, span, planes, cells),
             vmem(rows, cells),
-            vmem(rows, cells),
+            vmem(8, cells),
+            vmem(8, cells),
+            vmem(planes, cells),
             vmem(chunks, planes, cells),
             vmem(ranks, 8, LANES),
             vmem(doms, 8, LANES),
-            dma((3 + count,)),
-            dma((CYCLES, 2)), dma((CYCLES, 2)),
-            dma((CYCLES, ranks)), dma((CYCLES, ranks)),
-            dma((CYCLES, span)), dma((CYCLES, span)),
-            dma((CYCLES, span)), dma((CYCLES, span)),
-            dma((ranks,)), dma((ranks,)),
-            dma((doms,)), dma((doms,)),
-            dma((ranks,)), dma((chunks,)),
-            dma((2 * rim,)),
+            dma((4,)),
+            dma((CYCLES,)), dma((CYCLES, 2)),
+            dma((CYCLES,)), dma((CYCLES,)),
+            dma((CYCLES,)), dma((CYCLES,)),
+            dma((CYCLES,)), dma((CYCLES,)),
+            dma((1,)), dma((1,)),
+            dma((1,)), dma((1,)),
+            dma((1,)), dma((2 * rim + 1,)),
+            dma((1,)),
         ],
         compiler_params=pltpu.CompilerParams(collective_id=0, has_side_effects=True),
         name="cycles",

time: 54.9 us -> 53.6 us (0.976)
  Pallas kernels: 53.4 us -> 52.1 us
    pallas_call x1, Pallas kernels: 53.4 us -> 52.1 us  [body(): pl.pallas_call(functools.partial(cycles_kernel, doms, ranks), out_shape=p...]
where the time goes in v3:
time: 53.6 us; the launch traced here: 53.4 us
  Pallas kernels  52.1 us (97%)
  between operations  0.66 us (1%)
  local copies, waits for them, and re-layouts  0.62 us (1%)
    pallas_call x1, Pallas kernels, body(): pl.pallas_call(functools.partial(cycles_kernel, doms, ranks), out_shape=p...  52.1 us

profile of v3, /device:TPU:0, one launch (start us, length us, event | category | flops | bytes accessed | tf_op | source)
XLA Modules:
  0.0 53.4 jit_solution(1367170040639261076)
XLA Ops:
  0.7 52.1 %cycles.1 = f32[4,2304]{1,0:T(4,128)S(1)} custom-call(f32[2,48,2304]{2,1,0:T(8,128)} %bitcast.5, f32[1,2]{1,0:T(1,128)} %refs_1_.1, s32[1,1]{1,0:T(1,128)} %bitcast.4.refs_2_, f32[1,48]{1,0:T(1,128)} %refs_3_.1, f32[48,2304]{1,0:T(8,128)} %bitcast.6, f32[48,2304]{1,0:T(8,128)} %bitcast.7, f32[4,2304]{1,0:T(4,128)} %refs_6_.1), custom_call_target="tpu_custom_call" | custom-call | tf_op jit(solution)/shard_map/cycles/pallas_call | solution.py:594
  52.8 0.6 %copy.9 = f32[4,2304]{1,0:T(4,128)} copy(f32[4,2304]{1,0:T(4,128)S(1)} %cycles.1) | data formatting | bytes 73728

commit v4 on v3

--- a/solution.py
+++ b/solution.py
@@ -362,9 +362,8 @@
         if cycle == 0:
             pl.semaphore_wait(barrier, everyone - 1)
             guess.wait()
-            h_copies = near_copies(0, near_h, h_send, h_recv)
-            for copy in h_copies:
-                copy.start()
+        for copy in near_copies(cycle, near_h, h_send, h_recv):
+            copy.start()
 
         def two_steps(step, carry):
             filter_step(shape, odd, even, scale, inverse, False)
@@ -450,7 +449,17 @@
         def give(owner):
             part_copy(owner).start()
 
-        outward(rim, ranks - rim, give)
+        def delayed(owner):
+            apart = (2 * owner >= ranks) != (2 * rank >= ranks)
+            return jnp.logical_and(apart, lax.rem(owner + rank, 2) == 1)
+
+        def give_now(owner):
+            pl.when(jnp.logical_not(delayed(owner)))(lambda: give(owner))
+
+        def give_later(owner):
+            pl.when(delayed(owner))(lambda: give(owner))
+
+        outward(rim, ranks - rim, give_now)
         found = weigh(edges, found)
         if last:
             sums[rank] = found
@@ -467,6 +476,7 @@
                 pl.when(base + j != rank)(lambda: give(base + j))
 
         repeat(0, 2, join)
+        outward(rim, ranks - rim, give_later)
 
         arrived(near_h.at[cycle, : span - 1], h_recv.at[cycle])
         for slot in range(span):
@@ -525,9 +535,6 @@
 
             outward(0, ranks, lambda to: box_copy(to).start())
             near_h[cycle + 1, reach] = relaxed[2 : 2 + planes, :] + change
-            h_copies = near_copies(cycle + 1, near_h, h_send, h_recv)
-            for copy in h_copies:
-                copy.start()
 
             def relay_copy(index):
                 side, j = lax.div(index, rim), lax.rem(index, rim)

time: 53.6 us -> 52.5 us (0.979)
  Pallas kernels: 52.1 us -> 51 us
    pallas_call x1, Pallas kernels: 52.1 us -> 51 us  [body(): pl.pallas_call(functools.partial(cycles_kernel, doms, ranks), out_shape=p...]
where the time goes in v4:
time: 52.5 us; the launch traced here: 52.3 us
  Pallas kernels  51 us (97%)
  between operations  0.66 us (1%)
  local copies, waits for them, and re-layouts  0.62 us (1%)
    pallas_call x1, Pallas kernels, body(): pl.pallas_call(functools.partial(cycles_kernel, doms, ranks), out_shape=p...  51 us

profile of v4, /device:TPU:0, one launch (start us, length us, event | category | flops | bytes accessed | tf_op | source)
XLA Modules:
  0.0 52.3 jit_solution(15975439056640857969)
XLA Ops:
  0.7 51.0 %cycles.1 = f32[4,2304]{1,0:T(4,128)S(1)} custom-call(f32[2,48,2304]{2,1,0:T(8,128)} %bitcast.5, f32[1,2]{1,0:T(1,128)} %refs_1_.1, s32[1,1]{1,0:T(1,128)} %bitcast.4.refs_2_, f32[1,48]{1,0:T(1,128)} %refs_3_.1, f32[48,2304]{1,0:T(8,128)} %bitcast.6, f32[48,2304]{1,0:T(8,128)} %bitcast.7, f32[4,2304]{1,0:T(4,128)} %refs_6_.1), custom_call_target="tpu_custom_call" | custom-call | tf_op jit(solution)/shard_map/cycles/pallas_call | solution.py:601
  51.7 0.6 %copy.9 = f32[4,2304]{1,0:T(4,128)} copy(f32[4,2304]{1,0:T(4,128)S(1)} %cycles.1) | data formatting | bytes 73728

commit v5 on v4

--- a/solution.py
+++ b/solution.py
@@ -238,12 +238,14 @@
 
     barrier = pltpu.get_barrier_semaphore()
 
-    def greet(k):
-        pl.semaphore_signal(
-            barrier, inc=1, device_id=place(lax.rem(me + k, everyone)), device_id_type=MESH
-        )
-
-    repeat(1, everyone, greet)
+    def greet(to):
+        pl.semaphore_signal(barrier, inc=1, device_id=to, device_id_type=MESH)
+
+    repeat(1, ranks, lambda k: greet((dom, lax.rem(rank + k, ranks))))
+    repeat(1, doms, lambda k: greet((lax.rem(dom + k, doms), rank)))
+    for k in range(1, reach + 1):
+        greet(place(lax.rem(me + k, everyone)))
+        greet(place(lax.rem(me - k + everyone, everyone)))
 
     sublane = lax.broadcasted_iota(jnp.int32, (8, LANES), 0)
     for group in range(0, box, 8):
@@ -360,7 +362,7 @@
 
         filter_step(shape, even, odd, scale, inverse, True)
         if cycle == 0:
-            pl.semaphore_wait(barrier, everyone - 1)
+            pl.semaphore_wait(barrier, ranks + doms - 2 + 2 * reach)
             guess.wait()
         for copy in near_copies(cycle, near_h, h_send, h_recv):
             copy.start()

time: 52.5 us -> 51.1 us (0.973)
  Pallas kernels: 51 us -> 49.6 us
    pallas_call x1, Pallas kernels: 51 us -> 49.6 us  [body(): pl.pallas_call(functools.partial(cycles_kernel, doms, ranks), out_shape=p...]
where the time goes in v5:
time: 51.1 us; the launch traced here: 50.9 us
  Pallas kernels  49.6 us (97%)
  between operations  0.66 us (1%)
  local copies, waits for them, and re-layouts  0.62 us (1%)
    pallas_call x1, Pallas kernels, body(): pl.pallas_call(functools.partial(cycles_kernel, doms, ranks), out_shape=p...  49.6 us

profile of v5, /device:TPU:0, one launch (start us, length us, event | category | flops | bytes accessed | tf_op | source)
XLA Modules:
  0.0 50.9 jit_solution(4109138628234375917)
XLA Ops:
  0.7 49.6 %cycles.1 = f32[4,2304]{1,0:T(4,128)S(1)} custom-call(f32[2,48,2304]{2,1,0:T(8,128)} %bitcast.5, f32[1,2]{1,0:T(1,128)} %refs_1_.1, s32[1,1]{1,0:T(1,128)} %bitcast.4.refs_2_, f32[1,48]{1,0:T(1,128)} %refs_3_.1, f32[48,2304]{1,0:T(8,128)} %bitcast.6, f32[48,2304]{1,0:T(8,128)} %bitcast.7, f32[4,2304]{1,0:T(4,128)} %refs_6_.1), custom_call_target="tpu_custom_call" | custom-call | tf_op jit(solution)/shard_map/cycles/pallas_call | solution.py:603
  50.3 0.6 %copy.9 = f32[4,2304]{1,0:T(4,128)} copy(f32[4,2304]{1,0:T(4,128)S(1)} %cycles.1) | data formatting | bytes 73728

commit v6 on v5

--- a/solution.py
+++ b/solution.py
@@ -234,7 +234,6 @@
         loads(orbitals_hbm.at[orbital], planes_of.at[orbital], load_sem.at[1])
     guess = pltpu.make_async_copy(hartree_hbm, near_h.at[0, reach], load_sem.at[2])
     guess.start()
-    loads(core_hbm, core, load_sem.at[3])
 
     barrier = pltpu.get_barrier_semaphore()
 
@@ -246,13 +245,6 @@
     for k in range(1, reach + 1):
         greet(place(lax.rem(me + k, everyone)))
         greet(place(lax.rem(me - k + everyone, everyone)))
-
-    sublane = lax.broadcasted_iota(jnp.int32, (8, LANES), 0)
-    for group in range(0, box, 8):
-        rows = jnp.full((8, LANES), weights[0, group], jnp.float32)
-        for row in range(1, 8):
-            rows = jnp.where(sublane == row, weights[0, group + row], rows)
-        weight_rows[group : group + 8, :] = rows
 
     lane = lax.broadcasted_iota(jnp.int32, (8, LANES), 1)
     orbital_of = lax.rem(lax.div(lane, shape.across), count)
@@ -363,9 +355,17 @@
         filter_step(shape, even, odd, scale, inverse, True)
         if cycle == 0:
             pl.semaphore_wait(barrier, ranks + doms - 2 + 2 * reach)
+            loads(core_hbm, core, load_sem.at[3])
             guess.wait()
         for copy in near_copies(cycle, near_h, h_send, h_recv):
             copy.start()
+        if cycle == 0:
+            sublane = lax.broadcasted_iota(jnp.int32, (8, LANES), 0)
+            for group in range(0, box, 8):
+                rows = jnp.full((8, LANES), weights[0, group], jnp.float32)
+                for row in range(1, 8):
+                    rows = jnp.where(sublane == row, weights[0, group + row], rows)
+                weight_rows[group : group + 8, :] = rows
 
         def two_steps(step, carry):
             filter_step(shape, odd, even, scale, inverse, False)
@@ -453,7 +453,7 @@
 
         def delayed(owner):
             apart = (2 * owner >= ranks) != (2 * rank >= ranks)
-            return jnp.logical_and(apart, lax.rem(owner + rank, 2) == 1)
+            return jnp.logical_and(apart, lax.rem(owner + rank, 2) == 0)
 
         def give_now(owner):
             pl.when(jnp.logical_not(delayed(owner)))(lambda: give(owner))

time: 51.1 us -> 50.8 us (level)
  no operation moved by 1% of the time
where the time goes in v6:
time: 50.8 us; the launch traced here: 50.6 us
  Pallas kernels  49.3 us (97%)
  between operations  0.66 us (1%)
  local copies, waits for them, and re-layouts  0.62 us (1%)
    pallas_call x1, Pallas kernels, body(): pl.pallas_call(functools.partial(cycles_kernel, doms, ranks), out_shape=p...  49.3 us

profile of v6, /device:TPU:0, one launch (start us, length us, event | category | flops | bytes accessed | tf_op | source)
XLA Modules:
  0.0 50.6 jit_solution(3624622279540514468)
XLA Ops:
  0.7 49.3 %cycles.1 = f32[4,2304]{1,0:T(4,128)S(1)} custom-call(f32[2,48,2304]{2,1,0:T(8,128)} %bitcast.5, f32[1,2]{1,0:T(1,128)} %refs_1_.1, s32[1,1]{1,0:T(1,128)} %bitcast.4.refs_2_, f32[1,48]{1,0:T(1,128)} %refs_3_.1, f32[48,2304]{1,0:T(8,128)} %bitcast.6, f32[48,2304]{1,0:T(8,128)} %bitcast.7, f32[4,2304]{1,0:T(4,128)} %refs_6_.1), custom_call_target="tpu_custom_call" | custom-call | tf_op jit(solution)/shard_map/cycles/pallas_call | solution.py:603
  49.9 0.6 %copy.9 = f32[4,2304]{1,0:T(4,128)} copy(f32[4,2304]{1,0:T(4,128)S(1)} %cycles.1) | data formatting | bytes 73728
